TPU v7x, 32 devices: a whole 2x2x4 slice. The times are simulated.
32 devices in a mesh: level: 2 (over core), gx: 4 (over y, x), yz: 4 (over z).
Axes of the slice: x: 2, y: 2, z: 4, core: 2. Of those that a mesh axis runs over, the one named last changes fastest.
Arguments:
- init_field: float32 [128, 64, 256], P('gx', 'yz'), may hold values from -6 to 6
- source: float32 [128, 64, 256], P('gx', 'yz'), may hold values from -4 to 4
- damping: float32 [128, 64, 256], P('gx', 'yz'), may hold values from 0.05 to 2
Outputs:
- final_states: float32 [2, 128, 64, 256], P('level', 'gx', 'yz')
All inputs are finite; a program needn't handle non-finite values.
Results may differ from a plain program's by a relative error of at most 0.0001.
Values sent between devices are 32-bit elements; how exact they have to be, the bound alone decides.
A program may use at most 64 MiB of HBM per device.

v0:
```python
import functools

import jax
import jax.numpy as jnp
from jax import lax
from jax.experimental import pallas as pl
from jax.experimental.pallas import tpu as pltpu
from jax.sharding import PartitionSpec as P

STEPS = 3
ITERS = 3
PX = 3
PY = 8
LANES = 128
MID = 8.025
HALF = 6.975
MESH = pl.DeviceIdType.MESH
DIRS = ((-1, 0), (1, 0), (0, -1), (0, 1), (-1, -1), (-1, 1), (1, -1), (1, 1))


def times_a(c):
    out = [MID * v for v in c] + [jnp.zeros_like(c[0])]
    for k, v in enumerate(c):
        if k == 0:
            out[1] = out[1] + HALF * v
        else:
            out[k + 1] = out[k + 1] + (0.5 * HALF) * v
            out[k - 1] = out[k - 1] + (0.5 * HALF) * v
    return out


def plus(a, b):
    short, long = (a, b) if len(a) < len(b) else (b, a)
    return [x + y for x, y in zip(short, long)] + long[len(short):]


def scaled(s, a):
    return [s * x for x in a]


def cg_coefficients(dots):
    m = [dots[0], dots[1], 2.0 * dots[2] - dots[0], 2.0 * dots[3] - dots[1],
         2.0 * dots[4] - dots[0], 2.0 * dots[5] - dots[1]]

    def inner(a, b):
        total = None
        for i, x in enumerate(a):
            for j, y in enumerate(b):
                term = (x * y) * (0.5 * (m[i + j] + m[abs(i - j)]))
                total = term if total is None else total + term
        return total

    one = jnp.ones_like(m[0])
    resid = [one]
    direction = resid
    image = times_a(resid)
    along = image
    norm_now = m[0]
    alpha = norm_now / inner(resid, image)
    answer = None
    for step in range(ITERS):
        move = scaled(alpha, direction)
        answer = move if answer is None else plus(answer, move)
        if step + 1 < ITERS:
            resid = plus(resid, scaled(-alpha, along))
            image = times_a(resid)
            norm_next = inner(resid, resid)
            product = inner(resid, image)
            ratio = norm_next / norm_now
            alpha = norm_next / (product - ratio * norm_next / alpha)
            direction = plus(resid, scaled(ratio, direction))
            along = plus(image, scaled(ratio, along))
            norm_now = norm_next
    change = plus(times_a(answer), scaled(-1.0, answer))
    return answer, change


def body(sizes, stages, init_ref, source_ref, damp_ref, out_ref, p0, src, dmp, heads_p, heads_c,
         work_p, work_c, ahead, base, sums, result, inbox, slots, in_sem, send_sem, recv_sem, red_send, red_recv, out_sem):
    levels, nx, ny = sizes
    half = src.shape[0]
    parts = src.shape[1]
    rows = src.shape[2]
    level, gx, yz = lax.axis_index("level"), lax.axis_index("gx"), lax.axis_index("yz")
    xpos = gx * levels + level
    xcount = nx * levels
    x_in = (xpos > 0, xpos < xcount - 1)
    y_in = (yz > 0, yz < ny - 1)

    def exists(dx, dy):
        ok = None
        for d, pair in ((dx, x_in), (dy, y_in)):
            if d != 0:
                c = pair[0] if d < 0 else pair[1]
                ok = c if ok is None else jnp.logical_and(ok, c)
        return ok

    mine = pl.ds(level * half, half)
    loads = []
    for i, (ref, buf, pad) in enumerate(((init_ref, p0, True), (damp_ref, dmp, True), (source_ref, src, False))):
        for z in range(parts):
            lanes = slice(z * LANES, (z + 1) * LANES)
            dst = buf.at[PX:PX + half, z, PY:PY + rows, :] if pad else buf.at[:, z, :, :]
            copy = pltpu.make_async_copy(ref.at[mine, :, lanes], dst, in_sem.at[i, z])
            copy.start()
            loads.append(copy)

    zero_x = jnp.zeros((PX,) + tuple(p0.shape[1:]), jnp.float32)
    zero_y = jnp.zeros((p0.shape[0], parts, PY, LANES), jnp.float32)
    for buf in [p0] + [h.at[n] for h in (heads_p, heads_c) for n in range(STEPS)]:
        @pl.when(jnp.logical_not(x_in[0]))
        def _(buf=buf):
            buf[0:PX] = zero_x

        @pl.when(jnp.logical_not(x_in[1]))
        def _(buf=buf):
            buf[PX + half:] = zero_x

        @pl.when(jnp.logical_not(y_in[0]))
        def _(buf=buf):
            buf[:, :, 0:PY, :] = zero_y

        @pl.when(jnp.logical_not(y_in[1]))
        def _(buf=buf):
            buf[:, :, PY + rows:, :] = zero_y

    def halo_copy(buf, width, slot, k, into=None):
        dx, dy = DIRS[k]
        w = width if 0 in (dx, dy) else width - 1
        if w == 0:
            return None

        def spans(d, pad, size):
            if d == 0:
                return slice(pad, pad + size), slice(pad, pad + size)
            if d < 0:
                return slice(pad, pad + w), slice(pad + size, pad + size + w)
            return slice(pad + size - w, pad + size), slice(pad - w, pad)

        sx, tx = spans(dx, PX, half)
        sy, ty = spans(dy, PY, rows)
        to = xpos + dx
        return pltpu.make_async_remote_copy(
            src_ref=buf.at[sx, :, sy, :], dst_ref=(buf if into is None else into).at[tx, :, ty, :],
            send_sem=send_sem.at[slot, k], recv_sem=recv_sem.at[slot, k],
            device_id={"level": lax.rem(to + levels, levels), "gx": lax.div(to + levels, levels) - 1, "yz": yz + dy},
            device_id_type=MESH,
        )

    order = (4, 5, 6, 7, 2, 3, 0, 1)

    def send_halo(buf, width, slot, into=None):
        for k in order:
            copy = halo_copy(buf, width, slot, k, into)
            if copy is not None:
                pl.when(exists(*DIRS[k]))(lambda copy=copy: copy.start())

    def wait_halo(buf, width, slot, into=None):
        for k in order:
            copy = halo_copy(buf, width, slot, k, into)
            if copy is not None:
                dx, dy = DIRS[k]
                pl.when(exists(-dx, -dy))(lambda copy=copy: copy.wait_recv())

    def end_halo(buf, width, slot, into=None):
        for k in order:
            copy = halo_copy(buf, width, slot, k, into)
            if copy is not None:
                pl.when(exists(*DIRS[k]))(lambda copy=copy: copy.wait_send())

    def stencil(v, x, start, count):
        lane = lax.broadcasted_iota(jnp.int32, (count, LANES), 1)
        own = pl.ds(start, count)
        centre = [v[x, z, own, :] for z in range(parts)]
        fore = [pltpu.roll(c, 1, 1) for c in centre]
        back = [pltpu.roll(c, LANES - 1, 1) for c in centre]
        out = []
        for z in range(parts):
            near = jnp.where(lane == 0, fore[z - 1] if z > 0 else 0.0, fore[z])
            far = jnp.where(lane == LANES - 1, back[z + 1] if z + 1 < parts else 0.0, back[z])
            beside = v[x - 1, z, own, :] + v[x + 1, z, own, :]
            beside = beside + v[x, z, pl.ds(start - 1, count), :] + v[x, z, pl.ds(start + 1, count), :]
            beside = beside + (near + far)
            out.append((dmp[x, z, own, :] + (7.0 - MID)) * centre[z] - beside)
        return out, centre

    low = jnp.where(y_in[0], 0, PY)
    high = jnp.where(y_in[1], 2 * PY + rows, PY + rows)

    def fold(block):
        return jnp.sum(block.reshape(-1, 8, LANES), axis=0)

    def powers(head, work):
        zero = jnp.zeros((8, LANES), jnp.float32)
        own = pl.ds(PY, rows)
        totals = []
        for k in range(1, ITERS + 1):
            h = ITERS - k
            start = PY - h
            count = -(-(rows + 2 * h) // 8) * 8
            prev = head if k == 1 else work.at[k - 2]
            row = lax.broadcasted_iota(jnp.int32, (count, LANES), 0) + start

            mask = jnp.logical_and(row >= low, row < high)
            keep = jnp.logical_and(row >= PY, row < PY + rows)
            older = None if k == 1 else head if k == 2 else work.at[k - 3]

            def plane(x, inner, sides, k=k, h=h, start=start, count=count, prev=prev, mask=mask, keep=keep, older=older):
                a, b = sides
                t, centre = stencil(prev, x, start, count)
                ok = mask
                if not inner:
                    ok = jnp.logical_and(mask, x_in[0] if x < PX else x_in[1])
                for z in range(parts):
                    if k == 1:
                        new = t[z] * (1.0 / HALF)
                    else:
                        new = t[z] * (2.0 / HALF) - older[x, z, pl.ds(start, count), :]
                    if h > 0:
                        new = jnp.where(ok, new, 0.0)
                    work[k - 1, x, z, pl.ds(start, count), :] = new
                    if inner:
                        square, cross = centre[z] * centre[z], centre[z] * new
                        if h > 0:
                            square, cross = jnp.where(keep, square, 0.0), jnp.where(keep, cross, 0.0)
                        a = a + fold(square)
                        b = b + fold(cross)
                return a, b

            sides = (zero, zero)
            for x in range(PX - h, PX + half + h):
                sides = plane(x, PX <= x < PX + half, sides)
            totals += sides
        return totals

    def position(axes):
        flat = 0
        for a in axes:
            flat = flat * lax.axis_size(a) + lax.axis_index(a)
        return flat

    def reduce_all(accs, turn, meanwhile):
        n = len(accs)
        size = -(-n // 8) * 8
        eye = lax.broadcasted_iota(jnp.int32, (size, LANES), 0) == lax.broadcasted_iota(jnp.int32, (size, LANES), 1)
        tall = jnp.concatenate([jnp.sum(a, axis=0, keepdims=True) for a in accs]
                               + [jnp.zeros((size - n, LANES), jnp.float32)] * (size > n), axis=0)
        col = jnp.sum(tall, axis=1, keepdims=True)
        line = jnp.sum(jnp.where(eye, col, 0.0), axis=0, keepdims=True)
        for s, axes in enumerate(stages):
            count = 1
            for a in axes:
                count *= lax.axis_size(a)
            me = position(axes)
            cell = slots[s].at[turn, pl.ds(me, 1), :]
            cell[...] = line
            copies = []
            for off in range(1, count):
                peer = lax.rem(me + off, count)
                ids = {}
                for a in reversed(axes):
                    ids[a] = lax.rem(peer, lax.axis_size(a))
                    peer = lax.div(peer, lax.axis_size(a))
                copy = pltpu.make_async_remote_copy(
                    src_ref=cell, dst_ref=cell, send_sem=red_send[s].at[turn, off - 1],
                    recv_sem=red_recv[s].at[turn, off - 1], device_id=ids, device_id_type=MESH)
                copy.start()
                copies.append(copy)
            if s == 0:
                for item in meanwhile:
                    send_halo(*item)
            for copy in copies:
                copy.wait_recv()
            line = jnp.sum(slots[s][turn], axis=0, keepdims=True)
            for copy in copies:
                copy.wait_send()
        col = jnp.sum(jnp.where(eye, line, 0.0), axis=1, keepdims=True)
        wide = jnp.broadcast_to(col, (size, LANES))
        return [wide[k:k + 1, :] for k in range(n)]

    def to_out(block, part, row):
        return [pltpu.make_async_copy(
            block.at[:, z, :, :], out_ref.at[0, pl.ds(part * half, half), :, slice(z * LANES, (z + 1) * LANES)],
            out_sem.at[row, z]) for z in range(parts)]

    def pieces(f):
        return to_out(result.at[f], level, 2)

    def across(f):
        return pltpu.make_async_remote_copy(
            src_ref=result.at[f], dst_ref=inbox, send_sem=out_sem.at[0, 0], recv_sem=out_sem.at[1, 0],
            device_id={"level": f, "gx": gx, "yz": yz}, device_id_type=MESH)

    def deliver(f):
        pl.when(level != f)(lambda: across(f).start())
        for copy in pieces(f):
            pl.when(level == f)(lambda copy=copy: copy.start())

    own = pl.ds(PY, rows)
    for copy in loads[:2 * parts]:
        copy.wait()
    send_halo(p0, 1, 0)
    send_halo(dmp, ITERS - 1, 1)
    for copy in loads[2 * parts:]:
        copy.wait()
    wait_halo(p0, 1, 0)

    def start_plane(x, carry):
        t, centre = stencil(p0, x, PY, rows)
        for z in range(parts):
            r = src[x - PX, z] - (t[z] + (MID - 1.0) * centre[z])
            heads_p[0, x, z, own, :] = r
            base[x - PX, z] = r
        return carry

    lax.fori_loop(PX, PX + half, start_plane, 0, unroll=True)

    pending = [(p0, 1, 0), (dmp, ITERS - 1, 1)]
    slot = 2
    for turn in range(STEPS + 1):
        with_p, with_c = turn < STEPS, turn > 0
        fields = []
        if with_p:
            fields.append((heads_p.at[turn], work_p))
        if with_c:
            fields.append((heads_c.at[turn - 1], work_c))
        slots_here = []
        for head, _ in fields:
            if turn != 1:
                send_halo(head, ITERS, slot)
                slots_here.append((head, ITERS, slot))
                slot += 1
        if turn == 0:
            wait_halo(dmp, ITERS - 1, 1)
        accs = []
        for i, (head, work) in enumerate(fields):
            if turn != 1:
                wait_halo(*slots_here[i])
            accs += powers(head, work)
        pending += slots_here
        outer = []
        if turn == 0:
            for k in range(ITERS):
                outer.append((work_p.at[k], ITERS, slot, ahead.at[k]))
                slot += 1
            pending += outer
        dots = reduce_all(accs, turn, outer)
        coeff = [cg_coefficients(dots[6 * i:6 * i + 6]) for i in range(len(fields))]

        def update(i, carry, turn=turn, with_p=with_p, with_c=with_c, fields=fields, coeff=coeff):
            x = i + PX

            def basis(f, z):
                head, work = fields[f]
                return [head[x, z, own, :]] + [work[k, x, z, own, :] for k in range(ITERS)]

            def combine(c, v):
                total = c[0] * v[0]
                for a, b in zip(c[1:], v[1:]):
                    total = total + a * b
                return total

            for z in range(parts):
                line = base[i, z] if turn < STEPS else None
                if with_p:
                    v = basis(0, z)
                    rise = combine(coeff[0][0], v)
                    change = combine(coeff[0][1], v)
                    before = p0[x, z, own, :] if turn == 0 else sums[0, i, z]
                    if turn + 1 < STEPS:
                        sums[0, i, z] = before + rise
                        heads_p[turn + 1, x, z, own, :] = v[0] - change
                    else:
                        result[0, i, z] = before + rise
                if with_c:
                    v = basis(len(fields) - 1, z)
                    rise = combine(coeff[-1][0], v)
                    before = p0[x, z, own, :] if turn == 1 else sums[1, i, z]
                    if turn < STEPS:
                        sums[1, i, z] = before + rise
                        line = line - combine(coeff[-1][1], v)
                        base[i, z] = line
                    else:
                        result[1, i, z] = before + rise
                if turn < STEPS:
                    heads_c[turn, x, z, own, :] = line + 0.5 * change
            return carry

        lax.fori_loop(0, half, update, 0, unroll=True)
        if turn == 0:
            for item in outer:
                wait_halo(*item)
                end_halo(*item)
            pending = pending[:-len(outer)]

            def rim(x, begin, count, plane_ok):
                span = pl.ds(begin, count)
                row = lax.broadcasted_iota(jnp.int32, (count, LANES), 0) + begin
                ok = jnp.logical_and(row >= low, row < high)
                if plane_ok is not None:
                    ok = jnp.logical_and(ok, plane_ok)
                for z in range(parts):
                    now = heads_p[0, x, z, span, :]
                    change = coeff[0][1][0] * now
                    for k in range(ITERS):
                        change = change + coeff[0][1][k + 1] * ahead[k, x, z, span, :]
                    heads_p[1, x, z, span, :] = jnp.where(ok, now - change, 0.0)
                    heads_c[0, x, z, span, :] = jnp.where(ok, now + 0.5 * change, 0.0)

            for x in range(PX):
                rim(x, 0, 2 * PY + rows, x_in[0])
                rim(PX + half + x, 0, 2 * PY + rows, x_in[1])
            for x in range(PX, PX + half):
                rim(x, 0, PY, None)
                rim(x, PY + rows, PY, None)
        if turn == STEPS - 1:
            deliver(0)
    deliver(1)

    for item in pending:
        end_halo(*item)
    for f in range(2):
        pl.when(level != f)(lambda f=f: across(f).wait_send())
        pl.when(level == f)(lambda f=f: across(f).wait_recv())
        for copy in pieces(f):
            pl.when(level == f)(lambda copy=copy: copy.wait())
    ends = to_out(inbox, 1 - level, 3)
    for copy in ends:
        copy.start()
    for copy in ends:
        copy.wait()


def solution(mesh):
    levels, nx, ny = mesh.shape["level"], mesh.shape["gx"], mesh.shape["yz"]
    if levels * nx * ny <= 64:
        stages = (("level", "gx", "yz"),)
    else:
        stages = (("level", "gx"), ("yz",))

    def per_device(init_field, source, damping):
        deep, rows, wide = init_field.shape
        half, parts = deep // levels, wide // LANES
        padded = (half + 2 * PX, parts, rows + 2 * PY, LANES)
        plain = (half, parts, rows, LANES)
        counts = []
        for axes in stages:
            n = 1
            for a in axes:
                n *= mesh.shape[a]
            counts.append(n)
        turns = STEPS + 1
        dma = pltpu.SemaphoreType.DMA
        exchanges = 2 + 2 * STEPS + ITERS
        return pl.pallas_call(
            functools.partial(body, (levels, nx, ny), stages),
            out_shape=jax.ShapeDtypeStruct((1, deep, rows, wide), jnp.float32),
            in_specs=[pl.BlockSpec(memory_space=pl.ANY)] * 3,
            out_specs=pl.BlockSpec(memory_space=pl.ANY),
            scratch_shapes=[
                pltpu.VMEM(padded, jnp.float32),
                pltpu.VMEM(plain, jnp.float32),
                pltpu.VMEM(padded, jnp.float32),
                pltpu.VMEM((STEPS,) + padded, jnp.float32),
                pltpu.VMEM((STEPS,) + padded, jnp.float32),
                pltpu.VMEM((ITERS,) + padded, jnp.float32),
                pltpu.VMEM((ITERS,) + padded, jnp.float32),
                pltpu.VMEM((ITERS,) + padded, jnp.float32),
                pltpu.VMEM(plain, jnp.float32),
                pltpu.VMEM((2,) + plain, jnp.float32),
                pltpu.VMEM((2,) + plain, jnp.float32),
                pltpu.VMEM(plain, jnp.float32),
                [pltpu.VMEM((turns, n, LANES), jnp.float32) for n in counts],
                dma((3, parts)),
                dma((exchanges, 8)),
                dma((exchanges, 8)),
                [dma((turns, n - 1)) for n in counts],
                [dma((turns, n - 1)) for n in counts],
                dma((4, parts)),
            ],
            compiler_params=pltpu.CompilerParams(has_side_effects=True),
        )(init_field, source, damping)

    spec = P("gx", "yz", None)
    return jax.shard_map(
        per_device, mesh=mesh, in_specs=(spec, spec, spec),
        out_specs=P("level", "gx", "yz", None), check_vma=False,
    )
```

profile of v0, /device:TPU:0, one launch (start us, length us, event | category | flops | bytes accessed | tf_op | source)
XLA Modules:
  0.0 56.0 jit_solution(17339958370627739105)
XLA Ops:
  0.0 54.2 %shard_map.37 = f32[1,32,16,256]{3,2,1,0:T(8,128)} custom-call(f32[32,16,256]{2,1,0:T(8,128)} %init_ref.1, f32[32,16,256]{2,1,0:T(8,128)} %source_ref.1, f32[32,16,256]{2,1,0:T(8,128)} %damp_ref.1), custom_call_target="tpu_custom_call" | custom-call | tf_op jit(solution)/shard_map/pallas_call | solution.py:455
  54.2 1.9 %copy.5 = f32[1,32,16,256]{3,2,1,0:T(8,128)} copy(f32[1,32,16,256]{3,2,1,0:T(8,128)} %shard_map.37) | data formatting | bytes 1048576
where the time goes:
time: 56.2 us; the launch traced here: 56 us
  Pallas kernels  54.2 us (96%)
  local copies, waits for them, and re-layouts  1.87 us (3%)
    pallas_call x1, Pallas kernels, per_device(): pl.pallas_call(functools.partial(body, (levels, nx, ny), stages), out_sha...  54.2 us
    unnamed x1, local copies, waits for them, and re-layouts  1.87 us

commit v1 on v0

--- a/solution.py
+++ b/solution.py
@@ -95,6 +95,30 @@
                 ok = c if ok is None else jnp.logical_and(ok, c)
         return ok
 
+    def neighbour(dx, dy):
+        to = xpos + dx
+        return {"level": lax.rem(to + levels, levels), "gx": lax.div(to + levels, levels) - 1, "yz": yz + dy}
+
+    def position(axes):
+        flat = 0
+        for a in axes:
+            flat = flat * lax.axis_size(a) + lax.axis_index(a)
+        return flat
+
+    def others(axes):
+        count = 1
+        for a in axes:
+            count *= lax.axis_size(a)
+        found = []
+        for off in range(1, count):
+            peer = lax.rem(position(axes) + off, count)
+            ids = {}
+            for a in reversed(axes):
+                ids[a] = lax.rem(peer, lax.axis_size(a))
+                peer = lax.div(peer, lax.axis_size(a))
+            found.append(ids)
+        return found
+
     mine = pl.ds(level * half, half)
     loads = []
     for i, (ref, buf, pad) in enumerate(((init_ref, p0, True), (damp_ref, dmp, True), (source_ref, src, False))):
@@ -105,6 +129,18 @@
             copy.start()
             loads.append(copy)
 
+    barrier = pltpu.get_barrier_semaphore()
+    greeted = 0
+    for axes in stages:
+        for ids in others(axes):
+            pl.semaphore_signal(barrier, inc=1, device_id=ids, device_id_type=MESH)
+            greeted += 1
+    if len(stages) > 1:
+        for dx, dy in DIRS[4:]:
+            @pl.when(exists(dx, dy))
+            def _(dx=dx, dy=dy):
+                pl.semaphore_signal(barrier, inc=1, device_id=neighbour(dx, dy), device_id_type=MESH)
+
     zero_x = jnp.zeros((PX,) + tuple(p0.shape[1:]), jnp.float32)
     zero_y = jnp.zeros((p0.shape[0], parts, PY, LANES), jnp.float32)
     for buf in [p0] + [h.at[n] for h in (heads_p, heads_c) for n in range(STEPS)]:
@@ -124,6 +160,11 @@
         def _(buf=buf):
             buf[:, :, PY + rows:, :] = zero_y
 
+    pl.semaphore_wait(barrier, greeted)
+    if len(stages) > 1:
+        for dx, dy in DIRS[4:]:
+            pl.when(exists(dx, dy))(lambda: pl.semaphore_wait(barrier, 1))
+
     def halo_copy(buf, width, slot, k, into=None):
         dx, dy = DIRS[k]
         w = width if 0 in (dx, dy) else width - 1
@@ -139,12 +180,10 @@
 
         sx, tx = spans(dx, PX, half)
         sy, ty = spans(dy, PY, rows)
-        to = xpos + dx
         return pltpu.make_async_remote_copy(
             src_ref=buf.at[sx, :, sy, :], dst_ref=(buf if into is None else into).at[tx, :, ty, :],
             send_sem=send_sem.at[slot, k], recv_sem=recv_sem.at[slot, k],
-            device_id={"level": lax.rem(to + levels, levels), "gx": lax.div(to + levels, levels) - 1, "yz": yz + dy},
-            device_id_type=MESH,
+            device_id=neighbour(dx, dy), device_id_type=MESH,
         )
 
     order = (4, 5, 6, 7, 2, 3, 0, 1)
@@ -233,12 +272,6 @@
             totals += sides
         return totals
 
-    def position(axes):
-        flat = 0
-        for a in axes:
-            flat = flat * lax.axis_size(a) + lax.axis_index(a)
-        return flat
-
     def reduce_all(accs, turn, meanwhile):
         n = len(accs)
         size = -(-n // 8) * 8
@@ -248,19 +281,10 @@
         col = jnp.sum(tall, axis=1, keepdims=True)
         line = jnp.sum(jnp.where(eye, col, 0.0), axis=0, keepdims=True)
         for s, axes in enumerate(stages):
-            count = 1
-            for a in axes:
-                count *= lax.axis_size(a)
-            me = position(axes)
-            cell = slots[s].at[turn, pl.ds(me, 1), :]
+            cell = slots[s].at[turn, pl.ds(position(axes), 1), :]
             cell[...] = line
             copies = []
-            for off in range(1, count):
-                peer = lax.rem(me + off, count)
-                ids = {}
-                for a in reversed(axes):
-                    ids[a] = lax.rem(peer, lax.axis_size(a))
-                    peer = lax.div(peer, lax.axis_size(a))
+            for off, ids in enumerate(others(axes), 1):
                 copy = pltpu.make_async_remote_copy(
                     src_ref=cell, dst_ref=cell, send_sem=red_send[s].at[turn, off - 1],
                     recv_sem=red_recv[s].at[turn, off - 1], device_id=ids, device_id_type=MESH)
@@ -478,7 +502,7 @@
                 [dma((turns, n - 1)) for n in counts],
                 dma((4, parts)),
             ],
-            compiler_params=pltpu.CompilerParams(has_side_effects=True),
+            compiler_params=pltpu.CompilerParams(has_side_effects=True, collective_id=0),
         )(init_field, source, damping)
 
     spec = P("gx", "yz", None)

time: 56.2 us -> 52 us (0.925)
  Pallas kernels: 54.2 us -> 50 us
    pallas_call x1, Pallas kernels: 54.2 us -> 50 us  [per_device(): pl.pallas_call(functools.partial(body, (levels, nx, ny), stages), out_sha...]
where the time goes in v1:
time: 52 us; the launch traced here: 51.9 us
  Pallas kernels  50 us (96%)
  local copies, waits for them, and re-layouts  1.87 us (4%)
    pallas_call x1, Pallas kernels, per_device(): pl.pallas_call(functools.partial(body, (levels, nx, ny), stages), out_sha...  50 us
    unnamed x1, local copies, waits for them, and re-layouts  1.87 us

profile of v1, /device:TPU:0, one launch (start us, length us, event | category | flops | bytes accessed | tf_op | source)
XLA Modules:
  0.0 51.9 jit_solution(559606580440527042)
XLA Ops:
  0.0 50.0 %shard_map.37 = f32[1,32,16,256]{3,2,1,0:T(8,128)} custom-call(f32[32,16,256]{2,1,0:T(8,128)} %init_ref.1, f32[32,16,256]{2,1,0:T(8,128)} %source_ref.1, f32[32,16,256]{2,1,0:T(8,128)} %damp_ref.1), custom_call_target="tpu_custom_call" | custom-call | tf_op jit(solution)/shard_map/pallas_call | solution.py:479
  50.0 1.9 %copy.5 = f32[1,32,16,256]{3,2,1,0:T(8,128)} copy(f32[1,32,16,256]{3,2,1,0:T(8,128)} %shard_map.37) | data formatting | bytes 1048576

commit v2 on v1

--- a/solution.py
+++ b/solution.py
@@ -15,6 +15,8 @@
 MID = 8.025
 HALF = 6.975
 MESH = pl.DeviceIdType.MESH
+NONE = (0, 0)
+EARLY = 1
 DIRS = ((-1, 0), (1, 0), (0, -1), (0, 1), (-1, -1), (-1, 1), (1, -1), (1, 1))
 
 
@@ -76,7 +78,7 @@
 
 
 def body(sizes, stages, init_ref, source_ref, damp_ref, out_ref, p0, src, dmp, heads_p, heads_c,
-         work_p, work_c, ahead, base, sums, result, inbox, slots, in_sem, send_sem, recv_sem, red_send, red_recv, out_sem):
+         works, ahead, base, sums, result, inbox, slots, in_sem, send_sem, recv_sem, red_send, red_recv, out_sem):
     levels, nx, ny = sizes
     half = src.shape[0]
     parts = src.shape[1]
@@ -130,11 +132,17 @@
             loads.append(copy)
 
     barrier = pltpu.get_barrier_semaphore()
+    reach = max(1, ny - 3) if len(stages) == 1 else ny
     greeted = 0
     for axes in stages:
         for ids in others(axes):
-            pl.semaphore_signal(barrier, inc=1, device_id=ids, device_id_type=MESH)
-            greeted += 1
+            close = jnp.abs(ids.get("yz", yz) - yz) <= reach
+
+            @pl.when(close)
+            def _(ids=ids):
+                pl.semaphore_signal(barrier, inc=1, device_id=ids, device_id_type=MESH)
+
+            greeted = greeted + close.astype(jnp.int32)
     if len(stages) > 1:
         for dx, dy in DIRS[4:]:
             @pl.when(exists(dx, dy))
@@ -165,45 +173,47 @@
         for dx, dy in DIRS[4:]:
             pl.when(exists(dx, dy))(lambda: pl.semaphore_wait(barrier, 1))
 
-    def halo_copy(buf, width, slot, k, into=None):
+    def halo_copy(item, k):
+        buf, faces, corners, slot, into = item
         dx, dy = DIRS[k]
-        w = width if 0 in (dx, dy) else width - 1
-        if w == 0:
+        lo, hi = faces if 0 in (dx, dy) else corners
+        if hi == lo:
             return None
+        lead = (slice(None),) * (len(buf.shape) - 4)
 
         def spans(d, pad, size):
             if d == 0:
                 return slice(pad, pad + size), slice(pad, pad + size)
             if d < 0:
-                return slice(pad, pad + w), slice(pad + size, pad + size + w)
-            return slice(pad + size - w, pad + size), slice(pad - w, pad)
+                return slice(pad + lo, pad + hi), slice(pad + size + lo, pad + size + hi)
+            return slice(pad + size - hi, pad + size - lo), slice(pad - hi, pad - lo)
 
         sx, tx = spans(dx, PX, half)
         sy, ty = spans(dy, PY, rows)
         return pltpu.make_async_remote_copy(
-            src_ref=buf.at[sx, :, sy, :], dst_ref=(buf if into is None else into).at[tx, :, ty, :],
+            src_ref=buf.at[lead + (sx, slice(None), sy)], dst_ref=(buf if into is None else into).at[lead + (tx, slice(None), ty)],
             send_sem=send_sem.at[slot, k], recv_sem=recv_sem.at[slot, k],
             device_id=neighbour(dx, dy), device_id_type=MESH,
         )
 
     order = (4, 5, 6, 7, 2, 3, 0, 1)
 
-    def send_halo(buf, width, slot, into=None):
+    def send_halo(item):
         for k in order:
-            copy = halo_copy(buf, width, slot, k, into)
+            copy = halo_copy(item, k)
             if copy is not None:
                 pl.when(exists(*DIRS[k]))(lambda copy=copy: copy.start())
 
-    def wait_halo(buf, width, slot, into=None):
+    def wait_halo(item):
         for k in order:
-            copy = halo_copy(buf, width, slot, k, into)
+            copy = halo_copy(item, k)
             if copy is not None:
                 dx, dy = DIRS[k]
                 pl.when(exists(-dx, -dy))(lambda copy=copy: copy.wait_recv())
 
-    def end_halo(buf, width, slot, into=None):
+    def end_halo(item):
         for k in order:
-            copy = halo_copy(buf, width, slot, k, into)
+            copy = halo_copy(item, k)
             if copy is not None:
                 pl.when(exists(*DIRS[k]))(lambda copy=copy: copy.wait_send())
 
@@ -223,29 +233,28 @@
             out.append((dmp[x, z, own, :] + (7.0 - MID)) * centre[z] - beside)
         return out, centre
 
+    own = pl.ds(PY, rows)
     low = jnp.where(y_in[0], 0, PY)
     high = jnp.where(y_in[1], 2 * PY + rows, PY + rows)
 
     def fold(block):
         return jnp.sum(block.reshape(-1, 8, LANES), axis=0)
 
-    def powers(head, work):
+    def powers(fields, after):
         zero = jnp.zeros((8, LANES), jnp.float32)
-        own = pl.ds(PY, rows)
-        totals = []
+        totals = [[] for _ in fields]
         for k in range(1, ITERS + 1):
             h = ITERS - k
             start = PY - h
             count = -(-(rows + 2 * h) // 8) * 8
-            prev = head if k == 1 else work.at[k - 2]
             row = lax.broadcasted_iota(jnp.int32, (count, LANES), 0) + start
-
             mask = jnp.logical_and(row >= low, row < high)
             keep = jnp.logical_and(row >= PY, row < PY + rows)
-            older = None if k == 1 else head if k == 2 else work.at[k - 3]
-
-            def plane(x, inner, sides, k=k, h=h, start=start, count=count, prev=prev, mask=mask, keep=keep, older=older):
+
+            def plane(x, inner, sides, head, work):
                 a, b = sides
+                prev = head if k == 1 else work.at[k - 2]
+                older = None if k == 1 else head if k == 2 else work.at[k - 3]
                 t, centre = stencil(prev, x, start, count)
                 ok = mask
                 if not inner:
@@ -266,11 +275,26 @@
                         b = b + fold(cross)
                 return a, b
 
-            sides = (zero, zero)
-            for x in range(PX - h, PX + half + h):
-                sides = plane(x, PX <= x < PX + half, sides)
-            totals += sides
-        return totals
+            for (head, work), total in zip(fields, totals):
+                sides = (zero, zero)
+                for x in range(PX - h, PX + half + h):
+                    sides = plane(x, PX <= x < PX + half, sides, head, work)
+                total += sides
+            after(k)
+        return [v for total in totals for v in total]
+
+    def mixed(head, work, one, two):
+        sums_here = [jnp.zeros((8, LANES), jnp.float32)] * (2 * ITERS)
+        for x in range(PX, PX + half):
+            for z in range(parts):
+                last = head[x, z, own, :]
+                for k in range(ITERS):
+                    new = 1.5 * one[k, x, z, own, :] - 0.5 * two[k, x, z, own, :]
+                    work[k, x, z, own, :] = new
+                    sums_here[2 * k] = sums_here[2 * k] + fold(last * last)
+                    sums_here[2 * k + 1] = sums_here[2 * k + 1] + fold(last * new)
+                    last = new
+        return sums_here
 
     def reduce_all(accs, turn, meanwhile):
         n = len(accs)
@@ -292,7 +316,7 @@
                 copies.append(copy)
             if s == 0:
                 for item in meanwhile:
-                    send_halo(*item)
+                    item() if callable(item) else send_halo(item)
             for copy in copies:
                 copy.wait_recv()
             line = jnp.sum(slots[s][turn], axis=0, keepdims=True)
@@ -302,74 +326,180 @@
         wide = jnp.broadcast_to(col, (size, LANES))
         return [wide[k:k + 1, :] for k in range(n)]
 
-    def to_out(block, part, row):
-        return [pltpu.make_async_copy(
-            block.at[:, z, :, :], out_ref.at[0, pl.ds(part * half, half), :, slice(z * LANES, (z + 1) * LANES)],
-            out_sem.at[row, z]) for z in range(parts)]
-
-    def pieces(f):
-        return to_out(result.at[f], level, 2)
-
-    def across(f):
+    def across(f, part):
         return pltpu.make_async_remote_copy(
-            src_ref=result.at[f], dst_ref=inbox, send_sem=out_sem.at[0, 0], recv_sem=out_sem.at[1, 0],
+            src_ref=result.at[0], dst_ref=out_ref.at[0, pl.ds(part * half, half)], send_sem=out_sem.at[0, 0], recv_sem=out_sem.at[1, 0],
             device_id={"level": f, "gx": gx, "yz": yz}, device_id_type=MESH)
 
     def deliver(f):
-        pl.when(level != f)(lambda: across(f).start())
-        for copy in pieces(f):
-            pl.when(level == f)(lambda copy=copy: copy.start())
-
-    own = pl.ds(PY, rows)
+        @pl.when(level != f)
+        def _():
+            across(f, level).start()
+
+        @pl.when(level == f)
+        def _():
+            def keep(i, carry):
+                out_ref[0, level * half + i] = result[0, i]
+                return carry
+
+            lax.fori_loop(0, half, keep, 0, unroll=True)
+
+    def handed():
+        mine, last = slice(PX, PX + half), works.at[2 * STEPS - 1]
+        rows_here = slice(PY, PY + rows)
+        for n, (a, b) in enumerate((
+                (heads_c.at[STEPS - 1, mine, :, rows_here, :], inbox.at[0]),
+                (last.at[slice(0, ITERS - 1), mine, :, rows_here, :], inbox.at[slice(1, ITERS)]),
+                (sums.at[1], inbox.at[ITERS]))):
+            yield pltpu.make_async_remote_copy(
+                src_ref=a, dst_ref=b, send_sem=out_sem.at[0, 1 + n], recv_sem=out_sem.at[1, 1 + n],
+                device_id={"level": 1, "gx": gx, "yz": yz}, device_id_type=MESH)
+
+    def hand_over():
+        @pl.when(level == 0)
+        def _():
+            for copy in handed():
+                copy.start()
+
     for copy in loads[:2 * parts]:
         copy.wait()
-    send_halo(p0, 1, 0)
-    send_halo(dmp, ITERS - 1, 1)
+    first = [(p0, (0, 1), NONE, 0, None), (dmp, (0, ITERS - 1), (0, ITERS - 2), 1, None),
+             (heads_p.at[0], (0, ITERS), (0, ITERS - 1), 2, None)]
+    send_halo(first[0])
+    send_halo(first[1])
     for copy in loads[2 * parts:]:
         copy.wait()
-    wait_halo(p0, 1, 0)
+    wait_halo(first[0])
 
     def start_plane(x, carry):
         t, centre = stencil(p0, x, PY, rows)
         for z in range(parts):
-            r = src[x - PX, z] - (t[z] + (MID - 1.0) * centre[z])
-            heads_p[0, x, z, own, :] = r
-            base[x - PX, z] = r
+            heads_p[0, x, z, own, :] = src[x - PX, z] - (t[z] + (MID - 1.0) * centre[z])
         return carry
 
     lax.fori_loop(PX, PX + half, start_plane, 0, unroll=True)
 
-    pending = [(p0, 1, 0), (dmp, ITERS - 1, 1)]
-    slot = 2
+    send_halo(first[2])
+    wait_halo(first[1])
+    wait_halo(first[2])
+    pending = list(first)
+
+    def rim(turn, coeff, fields, far):
+        with_p, with_c = turn < STEPS, turn > 0
+
+        def piece(x, begin, count, plane_ok, valid):
+            span = pl.ds(begin, count)
+            row = lax.broadcasted_iota(jnp.int32, (count, LANES), 0) + begin
+            ok = jnp.logical_and(row >= low, row < high)
+            if plane_ok is not None:
+                ok = jnp.logical_and(ok, plane_ok)
+
+            def change(f, z):
+                total = coeff[f][1][0] * fields[f][0][x, z, span, :]
+                for k in range(1, ITERS + 1):
+                    near = valid(k, row)
+                    v = None
+                    for scale, work, wide in far[f]:
+                        if near is True:
+                            w = work[k - 1, x, z, span, :]
+                        else:
+                            w = wide[k - 1, x, z, span, :]
+                            if near is not False:
+                                w = jnp.where(near, work[k - 1, x, z, span, :], w)
+                        w = w if scale is None else scale * w
+                        v = w if v is None else v + w
+                    total = total + coeff[f][1][k] * v
+                return total
+
+            for z in range(parts):
+                rise = change(0, z)
+                line = heads_p[0, x, z, span, :] if turn < 2 else base[x, z, span, :]
+                if with_c:
+                    line = line - change(1, z)
+                    if turn + 1 < STEPS:
+                        base[x, z, span, :] = line
+                if turn + 1 < STEPS:
+                    heads_p[turn + 1, x, z, span, :] = jnp.where(ok, fields[0][0][x, z, span, :] - rise, 0.0)
+                heads_c[turn, x, z, span, :] = jnp.where(ok, line + 0.5 * rise, 0.0)
+
+        def below(k, row):
+            return False if k == ITERS else row >= PY - (ITERS - k)
+
+        def above(k, row):
+            return False if k == ITERS else row < PY + rows + (ITERS - k)
+
+        for x in range(PX, PX + half):
+            piece(x, 0, PY, None, below)
+            piece(x, PY + rows, PY, None, above)
+        for depth in range(1, PX + 1):
+            for x, there in ((PX - depth, x_in[0]), (PX + half + depth - 1, x_in[1])):
+                piece(x, PY, rows, there, lambda k, row: depth <= ITERS - k)
+                if depth < PX:
+                    piece(x, 0, PY, there, lambda k, row: False)
+                    piece(x, PY + rows, PY, there, lambda k, row: False)
+
+    slot = len(first)
+    used = 0
     for turn in range(STEPS + 1):
         with_p, with_c = turn < STEPS, turn > 0
         fields = []
         if with_p:
-            fields.append((heads_p.at[turn], work_p))
+            fields.append((heads_p.at[turn], works.at[used + len(fields)]))
         if with_c:
-            fields.append((heads_c.at[turn - 1], work_c))
-        slots_here = []
-        for head, _ in fields:
-            if turn != 1:
-                send_halo(head, ITERS, slot)
-                slots_here.append((head, ITERS, slot))
+            fields.append((heads_c.at[turn - 1], works.at[used + len(fields)]))
+        late, early, far = [], {}, None
+        if turn < STEPS:
+            sent = fields[:1] if turn == 1 else fields
+            these, there = slice(used, used + len(sent)), slice(used - (turn > 1), used - (turn > 1) + len(sent))
+            far = [((None, works.at[used + i], ahead.at[there.start + i]),) for i in range(len(sent))]
+            if turn == 1:
+                far.append(((1.5, works.at[0], ahead.at[0]), (-0.5, works.at[1], ahead.at[1])))
+            for k in range(1, ITERS + 1):
+                item = (works.at[these, k - 1], (ITERS - k, ITERS), NONE, slot, ahead.at[there, k - 1])
+                if turn == STEPS - 1 and k <= EARLY:
+                    early[k] = item
+                else:
+                    late.append(item)
                 slot += 1
-        if turn == 0:
-            wait_halo(dmp, ITERS - 1, 1)
-        accs = []
-        for i, (head, work) in enumerate(fields):
-            if turn != 1:
-                wait_halo(*slots_here[i])
-            accs += powers(head, work)
-        pending += slots_here
-        outer = []
-        if turn == 0:
-            for k in range(ITERS):
-                outer.append((work_p.at[k], ITERS, slot, ahead.at[k]))
-                slot += 1
-            pending += outer
-        dots = reduce_all(accs, turn, outer)
+            late.append((works.at[these], NONE, (0, ITERS - 1), slot, ahead.at[there]))
+            slot += 1
+        outer = list(early.values()) + late
+
+        def after(k, early=early):
+            if k in early:
+                send_halo(early[k])
+
+        if turn == 1:
+            accs = powers(fields[:1], after)
+            accs += mixed(fields[1][0], fields[1][1], works.at[0], works.at[1])
+        else:
+            accs = powers(fields, after)
+        pending += outer
+        dots = reduce_all(accs, turn, late if turn < STEPS else [hand_over])
         coeff = [cg_coefficients(dots[6 * i:6 * i + 6]) for i in range(len(fields))]
+
+        if turn == STEPS:
+            @pl.when(level == 1)
+            def _():
+                for copy in handed():
+                    copy.wait_recv()
+                c = coeff[-1][0]
+                last = works.at[2 * STEPS - 1]
+
+                def finish(i, carry):
+                    for z in range(parts):
+                        lanes = slice(z * LANES, (z + 1) * LANES)
+                        there, here = c[0] * inbox[0, i, z], c[0] * heads_c[STEPS - 1, i + PX, z, own, :]
+                        for k in range(1, ITERS):
+                            there = there + c[k] * inbox[k, i, z]
+                            here = here + c[k] * last[k - 1, i + PX, z, own, :]
+                        out_ref[0, i, :, lanes] = inbox[ITERS, i, z] + there
+                        out_ref[0, half + i, :, lanes] = sums[1, i, z] + here
+                    return carry
+
+                lax.fori_loop(0, half, finish, 0, unroll=True)
+
+            continue
 
         def update(i, carry, turn=turn, with_p=with_p, with_c=with_c, fields=fields, coeff=coeff):
             x = i + PX
@@ -385,7 +515,8 @@
                 return total
 
             for z in range(parts):
-                line = base[i, z] if turn < STEPS else None
+                lanes = slice(z * LANES, (z + 1) * LANES)
+                line = heads_p[0, x, z, own, :] if turn < 2 else base[x, z, own, :]
                 if with_p:
                     v = basis(0, z)
                     rise = combine(coeff[0][0], v)
@@ -395,64 +526,35 @@
                         sums[0, i, z] = before + rise
                         heads_p[turn + 1, x, z, own, :] = v[0] - change
                     else:
-                        result[0, i, z] = before + rise
+                        result[0, i, :, lanes] = before + rise
                 if with_c:
                     v = basis(len(fields) - 1, z)
                     rise = combine(coeff[-1][0], v)
                     before = p0[x, z, own, :] if turn == 1 else sums[1, i, z]
-                    if turn < STEPS:
-                        sums[1, i, z] = before + rise
-                        line = line - combine(coeff[-1][1], v)
-                        base[i, z] = line
-                    else:
-                        result[1, i, z] = before + rise
-                if turn < STEPS:
-                    heads_c[turn, x, z, own, :] = line + 0.5 * change
+                    sums[1, i, z] = before + rise
+                    line = line - combine(coeff[-1][1], v)
+                    if turn + 1 < STEPS:
+                        base[x, z, own, :] = line
+                heads_c[turn, x, z, own, :] = line + 0.5 * change
             return carry
 
         lax.fori_loop(0, half, update, 0, unroll=True)
-        if turn == 0:
-            for item in outer:
-                wait_halo(*item)
-                end_halo(*item)
-            pending = pending[:-len(outer)]
-
-            def rim(x, begin, count, plane_ok):
-                span = pl.ds(begin, count)
-                row = lax.broadcasted_iota(jnp.int32, (count, LANES), 0) + begin
-                ok = jnp.logical_and(row >= low, row < high)
-                if plane_ok is not None:
-                    ok = jnp.logical_and(ok, plane_ok)
-                for z in range(parts):
-                    now = heads_p[0, x, z, span, :]
-                    change = coeff[0][1][0] * now
-                    for k in range(ITERS):
-                        change = change + coeff[0][1][k + 1] * ahead[k, x, z, span, :]
-                    heads_p[1, x, z, span, :] = jnp.where(ok, now - change, 0.0)
-                    heads_c[0, x, z, span, :] = jnp.where(ok, now + 0.5 * change, 0.0)
-
-            for x in range(PX):
-                rim(x, 0, 2 * PY + rows, x_in[0])
-                rim(PX + half + x, 0, 2 * PY + rows, x_in[1])
-            for x in range(PX, PX + half):
-                rim(x, 0, PY, None)
-                rim(x, PY + rows, PY, None)
+        for item in outer:
+            wait_halo(item)
+        rim(turn, coeff, fields, far)
         if turn == STEPS - 1:
             deliver(0)
-    deliver(1)
-
+        used += len(fields)
     for item in pending:
-        end_halo(*item)
-    for f in range(2):
-        pl.when(level != f)(lambda f=f: across(f).wait_send())
-        pl.when(level == f)(lambda f=f: across(f).wait_recv())
-        for copy in pieces(f):
-            pl.when(level == f)(lambda copy=copy: copy.wait())
-    ends = to_out(inbox, 1 - level, 3)
-    for copy in ends:
-        copy.start()
-    for copy in ends:
-        copy.wait()
+        end_halo(item)
+
+    @pl.when(level == 0)
+    def _():
+        across(0, 1 - level).wait_recv()
+        for copy in handed():
+            copy.wait_send()
+
+    pl.when(level == 1)(lambda: across(0, level).wait_send())
 
 
 def solution(mesh):
@@ -475,32 +577,32 @@
             counts.append(n)
         turns = STEPS + 1
         dma = pltpu.SemaphoreType.DMA
-        exchanges = 2 + 2 * STEPS + ITERS
+        solves = 2 * STEPS
+        exchanges = 3 + STEPS * (1 + ITERS)
         return pl.pallas_call(
             functools.partial(body, (levels, nx, ny), stages),
-            out_shape=jax.ShapeDtypeStruct((1, deep, rows, wide), jnp.float32),
+            out_shape=pltpu.VMEM((1, deep, rows, wide), jnp.float32),
             in_specs=[pl.BlockSpec(memory_space=pl.ANY)] * 3,
-            out_specs=pl.BlockSpec(memory_space=pl.ANY),
+            out_specs=pl.BlockSpec(memory_space=pltpu.VMEM),
             scratch_shapes=[
                 pltpu.VMEM(padded, jnp.float32),
                 pltpu.VMEM(plain, jnp.float32),
                 pltpu.VMEM(padded, jnp.float32),
                 pltpu.VMEM((STEPS,) + padded, jnp.float32),
                 pltpu.VMEM((STEPS,) + padded, jnp.float32),
-                pltpu.VMEM((ITERS,) + padded, jnp.float32),
-                pltpu.VMEM((ITERS,) + padded, jnp.float32),
-                pltpu.VMEM((ITERS,) + padded, jnp.float32),
-                pltpu.VMEM(plain, jnp.float32),
+                pltpu.VMEM((solves, ITERS) + padded, jnp.float32),
+                pltpu.VMEM((solves - 2, ITERS) + padded, jnp.float32),
+                pltpu.VMEM(padded, jnp.float32),
                 pltpu.VMEM((2,) + plain, jnp.float32),
-                pltpu.VMEM((2,) + plain, jnp.float32),
-                pltpu.VMEM(plain, jnp.float32),
+                pltpu.VMEM((1, half, rows, wide), jnp.float32),
+                pltpu.VMEM((1 + ITERS,) + plain, jnp.float32),
                 [pltpu.VMEM((turns, n, LANES), jnp.float32) for n in counts],
                 dma((3, parts)),
                 dma((exchanges, 8)),
                 dma((exchanges, 8)),
                 [dma((turns, n - 1)) for n in counts],
                 [dma((turns, n - 1)) for n in counts],
-                dma((4, parts)),
+                dma((2, 4)),
             ],
             compiler_params=pltpu.CompilerParams(has_side_effects=True, collective_id=0),
         )(init_field, source, damping)

time: 52 us -> 44.8 us (0.86)
  Pallas kernels: 50 us -> 43.8 us
  local copies, waits for them, and re-layouts: 1.87 us -> 0.8 us
    pallas_call x1, Pallas kernels: 50 us -> 43.8 us  [per_device(): pl.pallas_call(functools.partial(body, (levels, nx, ny), stages), out_sha...]
    unnamed x1, local copies, waits for them, and re-layouts: 1.87 us -> 0.8 us
where the time goes in v2:
time: 44.8 us; the launch traced here: 44.6 us
  Pallas kernels  43.8 us (98%)
  local copies, waits for them, and re-layouts  0.8 us (2%)
    pallas_call x1, Pallas kernels, per_device(): pl.pallas_call(functools.partial(body, (levels, nx, ny), stages), out_sha...  43.8 us

profile of v2, /device:TPU:0, one launch (start us, length us, event | category | flops | bytes accessed | tf_op | source)
XLA Modules:
  0.0 44.6 jit_solution(14722160524855308204)
XLA Ops:
  0.0 43.8 %shard_map.37 = f32[1,32,16,256]{3,2,1,0:T(8,128)S(1)} custom-call(f32[32,16,256]{2,1,0:T(8,128)} %init_ref.1, f32[32,16,256]{2,1,0:T(8,128)} %source_ref.1, f32[32,16,256]{2,1,0:T(8,128)} %damp_ref.1), custom_call_target="tpu_custom_call" | custom-call | tf_op jit(solution)/shard_map/pallas_call | solution.py:582
  43.8 0.8 %copy.5 = f32[1,32,16,256]{3,2,1,0:T(8,128)} copy(f32[1,32,16,256]{3,2,1,0:T(8,128)S(1)} %shard_map.37) | data formatting | bytes 1048576

commit v3 on v2

--- a/solution.py
+++ b/solution.py
@@ -9,14 +9,15 @@
 
 STEPS = 3
 ITERS = 3
-PX = 3
+WIDTHS = (3, 3, 3, 3)
+PX = max(WIDTHS)
 PY = 8
 LANES = 128
 MID = 8.025
 HALF = 6.975
 MESH = pl.DeviceIdType.MESH
 NONE = (0, 0)
-EARLY = 1
+EARLY = (1, 1, 1)
 DIRS = ((-1, 0), (1, 0), (0, -1), (0, 1), (-1, -1), (-1, 1), (1, -1), (1, 1))
 
 
@@ -151,7 +152,7 @@
 
     zero_x = jnp.zeros((PX,) + tuple(p0.shape[1:]), jnp.float32)
     zero_y = jnp.zeros((p0.shape[0], parts, PY, LANES), jnp.float32)
-    for buf in [p0] + [h.at[n] for h in (heads_p, heads_c) for n in range(STEPS)]:
+    for buf in (p0, heads_p.at[0]):
         @pl.when(jnp.logical_not(x_in[0]))
         def _(buf=buf):
             buf[0:PX] = zero_x
@@ -240,11 +241,11 @@
     def fold(block):
         return jnp.sum(block.reshape(-1, 8, LANES), axis=0)
 
-    def powers(fields, after):
+    def powers(fields, extra, after):
         zero = jnp.zeros((8, LANES), jnp.float32)
         totals = [[] for _ in fields]
         for k in range(1, ITERS + 1):
-            h = ITERS - k
+            h = extra + ITERS - k
             start = PY - h
             count = -(-(rows + 2 * h) // 8) * 8
             row = lax.broadcasted_iota(jnp.int32, (count, LANES), 0) + start
@@ -363,8 +364,8 @@
 
     for copy in loads[:2 * parts]:
         copy.wait()
-    first = [(p0, (0, 1), NONE, 0, None), (dmp, (0, ITERS - 1), (0, ITERS - 2), 1, None),
-             (heads_p.at[0], (0, ITERS), (0, ITERS - 1), 2, None)]
+    first = [(p0, (0, 1), NONE, 0, None), (dmp, (0, PX - 1), (0, PX - 2), 1, None),
+             (heads_p.at[0], (0, WIDTHS[0]), (0, WIDTHS[0] - 1), 2, None)]
     send_halo(first[0])
     send_halo(first[1])
     for copy in loads[2 * parts:]:
@@ -385,7 +386,8 @@
     pending = list(first)
 
     def rim(turn, coeff, fields, far):
-        with_p, with_c = turn < STEPS, turn > 0
+        with_c = turn > 0
+        now, then = WIDTHS[turn], WIDTHS[turn + 1]
 
         def piece(x, begin, count, plane_ok, valid):
             span = pl.ds(begin, count)
@@ -422,21 +424,20 @@
                     heads_p[turn + 1, x, z, span, :] = jnp.where(ok, fields[0][0][x, z, span, :] - rise, 0.0)
                 heads_c[turn, x, z, span, :] = jnp.where(ok, line + 0.5 * rise, 0.0)
 
-        def below(k, row):
-            return False if k == ITERS else row >= PY - (ITERS - k)
-
-        def above(k, row):
-            return False if k == ITERS else row < PY + rows + (ITERS - k)
+        def near(k, layer):
+            if now - k >= then:
+                return True
+            return False if now == k else layer <= now - k
 
         for x in range(PX, PX + half):
-            piece(x, 0, PY, None, below)
-            piece(x, PY + rows, PY, None, above)
-        for depth in range(1, PX + 1):
+            piece(x, 0, PY, None, lambda k, row: near(k, PY - row))
+            piece(x, PY + rows, PY, None, lambda k, row: near(k, row - (PY + rows - 1)))
+        for depth in range(1, then + 1):
             for x, there in ((PX - depth, x_in[0]), (PX + half + depth - 1, x_in[1])):
-                piece(x, PY, rows, there, lambda k, row: depth <= ITERS - k)
-                if depth < PX:
-                    piece(x, 0, PY, there, lambda k, row: False)
-                    piece(x, PY + rows, PY, there, lambda k, row: False)
+                piece(x, PY, rows, there, lambda k, row: depth <= now - k)
+                if depth < then:
+                    piece(x, 0, PY, there, lambda k, row: now - k >= then)
+                    piece(x, PY + rows, PY, there, lambda k, row: now - k >= then)
 
     slot = len(first)
     used = 0
@@ -454,14 +455,17 @@
             far = [((None, works.at[used + i], ahead.at[there.start + i]),) for i in range(len(sent))]
             if turn == 1:
                 far.append(((1.5, works.at[0], ahead.at[0]), (-0.5, works.at[1], ahead.at[1])))
-            for k in range(1, ITERS + 1):
-                item = (works.at[these, k - 1], (ITERS - k, ITERS), NONE, slot, ahead.at[there, k - 1])
-                if turn == STEPS - 1 and k <= EARLY:
+            now, then = WIDTHS[turn], WIDTHS[turn + 1]
+            missing = [k for k in range(1, ITERS + 1) if now - k < then]
+            for k in missing:
+                item = (works.at[these, k - 1], (now - k, then), NONE, slot, ahead.at[there, k - 1])
+                if k <= EARLY[turn]:
                     early[k] = item
                 else:
                     late.append(item)
                 slot += 1
-            late.append((works.at[these], NONE, (0, ITERS - 1), slot, ahead.at[there]))
+            ks = slice(missing[0] - 1, ITERS)
+            late.append((works.at[these, ks], NONE, (0, then - 1), slot, ahead.at[there, ks]))
             slot += 1
         outer = list(early.values()) + late
 
@@ -469,11 +473,12 @@
             if k in early:
                 send_halo(early[k])
 
+        extra = WIDTHS[turn] - ITERS
         if turn == 1:
-            accs = powers(fields[:1], after)
+            accs = powers(fields[:1], extra, after)
             accs += mixed(fields[1][0], fields[1][1], works.at[0], works.at[1])
         else:
-            accs = powers(fields, after)
+            accs = powers(fields, extra, after)
         pending += outer
         dots = reduce_all(accs, turn, late if turn < STEPS else [hand_over])
         coeff = [cg_coefficients(dots[6 * i:6 * i + 6]) for i in range(len(fields))]

time: 44.8 us -> 44.6 us (level)
  no operation moved by 1% of the time
where the time goes in v3:
time: 44.6 us; the launch traced here: 44.4 us
  Pallas kernels  43.6 us (98%)
  local copies, waits for them, and re-layouts  0.8 us (2%)
    pallas_call x1, Pallas kernels, per_device(): pl.pallas_call(functools.partial(body, (levels, nx, ny), stages), out_sha...  43.6 us

profile of v3, /device:TPU:0, one launch (start us, length us, event | category | flops | bytes accessed | tf_op | source)
XLA Modules:
  0.0 44.4 jit_solution(10174503051490621428)
XLA Ops:
  0.0 43.6 %shard_map.37 = f32[1,32,16,256]{3,2,1,0:T(8,128)S(1)} custom-call(f32[32,16,256]{2,1,0:T(8,128)} %init_ref.1, f32[32,16,256]{2,1,0:T(8,128)} %source_ref.1, f32[32,16,256]{2,1,0:T(8,128)} %damp_ref.1), custom_call_target="tpu_custom_call" | custom-call | tf_op jit(solution)/shard_map/pallas_call | solution.py:587
  43.6 0.8 %copy.5 = f32[1,32,16,256]{3,2,1,0:T(8,128)} copy(f32[1,32,16,256]{3,2,1,0:T(8,128)S(1)} %shard_map.37) | data formatting | bytes 1048576

commit v4 on v3

--- a/solution.py
+++ b/solution.py
@@ -112,14 +112,23 @@
         count = 1
         for a in axes:
             count *= lax.axis_size(a)
+
+        def hops(off):
+            total = 0
+            for a in reversed(axes):
+                size = lax.axis_size(a)
+                total += min(off % size, size - off % size)
+                off //= size
+            return total
+
         found = []
-        for off in range(1, count):
+        for off in sorted(range(1, count), key=hops, reverse=True):
             peer = lax.rem(position(axes) + off, count)
             ids = {}
             for a in reversed(axes):
                 ids[a] = lax.rem(peer, lax.axis_size(a))
                 peer = lax.div(peer, lax.axis_size(a))
-            found.append(ids)
+            found.append((off, ids))
         return found
 
     mine = pl.ds(level * half, half)
@@ -136,7 +145,7 @@
     reach = max(1, ny - 3) if len(stages) == 1 else ny
     greeted = 0
     for axes in stages:
-        for ids in others(axes):
+        for _, ids in others(axes):
             close = jnp.abs(ids.get("yz", yz) - yz) <= reach
 
             @pl.when(close)
@@ -231,7 +240,7 @@
             beside = v[x - 1, z, own, :] + v[x + 1, z, own, :]
             beside = beside + v[x, z, pl.ds(start - 1, count), :] + v[x, z, pl.ds(start + 1, count), :]
             beside = beside + (near + far)
-            out.append((dmp[x, z, own, :] + (7.0 - MID)) * centre[z] - beside)
+            out.append((dmp[x, z, own, :], beside))
         return out, centre
 
     own = pl.ds(PY, rows)
@@ -250,7 +259,6 @@
             count = -(-(rows + 2 * h) // 8) * 8
             row = lax.broadcasted_iota(jnp.int32, (count, LANES), 0) + start
             mask = jnp.logical_and(row >= low, row < high)
-            keep = jnp.logical_and(row >= PY, row < PY + rows)
 
             def plane(x, inner, sides, head, work):
                 a, b = sides
@@ -261,19 +269,19 @@
                 if not inner:
                     ok = jnp.logical_and(mask, x_in[0] if x < PX else x_in[1])
                 for z in range(parts):
+                    rate, beside = t[z]
+                    new = rate * centre[z] - (2.0 / HALF) * beside
                     if k == 1:
-                        new = t[z] * (1.0 / HALF)
+                        new = 0.5 * new
                     else:
-                        new = t[z] * (2.0 / HALF) - older[x, z, pl.ds(start, count), :]
+                        new = new - older[x, z, pl.ds(start, count), :]
                     if h > 0:
                         new = jnp.where(ok, new, 0.0)
                     work[k - 1, x, z, pl.ds(start, count), :] = new
                     if inner:
-                        square, cross = centre[z] * centre[z], centre[z] * new
-                        if h > 0:
-                            square, cross = jnp.where(keep, square, 0.0), jnp.where(keep, cross, 0.0)
-                        a = a + fold(square)
-                        b = b + fold(cross)
+                        mid = centre[z] if h == 0 else prev[x, z, own, :]
+                        a = a + fold(mid * mid)
+                        b = b + fold(mid * (new if h == 0 else work[k - 1, x, z, own, :]))
                 return a, b
 
             for (head, work), total in zip(fields, totals):
@@ -309,7 +317,7 @@
             cell = slots[s].at[turn, pl.ds(position(axes), 1), :]
             cell[...] = line
             copies = []
-            for off, ids in enumerate(others(axes), 1):
+            for off, ids in others(axes):
                 copy = pltpu.make_async_remote_copy(
                     src_ref=cell, dst_ref=cell, send_sem=red_send[s].at[turn, off - 1],
                     recv_sem=red_recv[s].at[turn, off - 1], device_id=ids, device_id_type=MESH)
@@ -367,6 +375,13 @@
     first = [(p0, (0, 1), NONE, 0, None), (dmp, (0, PX - 1), (0, PX - 2), 1, None),
              (heads_p.at[0], (0, WIDTHS[0]), (0, WIDTHS[0] - 1), 2, None)]
     send_halo(first[0])
+
+    def scale(x, carry):
+        for z in range(parts):
+            dmp[x, z, own, :] = (dmp[x, z, own, :] + (7.0 - MID)) * (2.0 / HALF)
+        return carry
+
+    lax.fori_loop(PX, PX + half, scale, 0, unroll=True)
     send_halo(first[1])
     for copy in loads[2 * parts:]:
         copy.wait()
@@ -375,7 +390,8 @@
     def start_plane(x, carry):
         t, centre = stencil(p0, x, PY, rows)
         for z in range(parts):
-            heads_p[0, x, z, own, :] = src[x - PX, z] - (t[z] + (MID - 1.0) * centre[z])
+            rate, beside = t[z]
+            heads_p[0, x, z, own, :] = src[x - PX, z] - (((0.5 * HALF) * rate + (MID - 1.0)) * centre[z] - beside)
         return carry
 
     lax.fori_loop(PX, PX + half, start_plane, 0, unroll=True)
@@ -457,6 +473,9 @@
                 far.append(((1.5, works.at[0], ahead.at[0]), (-0.5, works.at[1], ahead.at[1])))
             now, then = WIDTHS[turn], WIDTHS[turn + 1]
             missing = [k for k in range(1, ITERS + 1) if now - k < then]
+            ks = slice(missing[0] - 1, ITERS)
+            late.append((works.at[these, ks], NONE, (0, then - 1), slot, ahead.at[there, ks]))
+            slot += 1
             for k in missing:
                 item = (works.at[these, k - 1], (now - k, then), NONE, slot, ahead.at[there, k - 1])
                 if k <= EARLY[turn]:
@@ -464,9 +483,6 @@
                 else:
                     late.append(item)
                 slot += 1
-            ks = slice(missing[0] - 1, ITERS)
-            late.append((works.at[these, ks], NONE, (0, then - 1), slot, ahead.at[there, ks]))
-            slot += 1
         outer = list(early.values()) + late
 
         def after(k, early=early):

time: 44.6 us -> 43.7 us (0.980)
  Pallas kernels: 43.6 us -> 42.7 us
    pallas_call x1, Pallas kernels: 43.6 us -> 42.7 us  [per_device(): pl.pallas_call(functools.partial(body, (levels, nx, ny), stages), out_sha...]
where the time goes in v4:
time: 43.7 us; the launch traced here: 43.5 us
  Pallas kernels  42.7 us (98%)
  local copies, waits for them, and re-layouts  0.8 us (2%)
    pallas_call x1, Pallas kernels, per_device(): pl.pallas_call(functools.partial(body, (levels, nx, ny), stages), out_sha...  42.7 us

profile of v4, /device:TPU:0, one launch (start us, length us, event | category | flops | bytes accessed | tf_op | source)
XLA Modules:
  0.0 43.5 jit_solution(18315962411063782295)
XLA Ops:
  0.0 42.7 %shard_map.37 = f32[1,32,16,256]{3,2,1,0:T(8,128)S(1)} custom-call(f32[32,16,256]{2,1,0:T(8,128)} %init_ref.1, f32[32,16,256]{2,1,0:T(8,128)} %source_ref.1, f32[32,16,256]{2,1,0:T(8,128)} %damp_ref.1), custom_call_target="tpu_custom_call" | custom-call | tf_op jit(solution)/shard_map/pallas_call | solution.py:603
  42.7 0.8 %copy.5 = f32[1,32,16,256]{3,2,1,0:T(8,128)} copy(f32[1,32,16,256]{3,2,1,0:T(8,128)S(1)} %shard_map.37) | data formatting | bytes 1048576

commit v5 on v4

--- a/solution.py
+++ b/solution.py
@@ -496,7 +496,7 @@
         else:
             accs = powers(fields, extra, after)
         pending += outer
-        dots = reduce_all(accs, turn, late if turn < STEPS else [hand_over])
+        dots = reduce_all(accs, turn, late + ([settle] if turn > 0 else []) + ([lambda: deliver(0), hand_over] if turn == STEPS else []))
         coeff = [cg_coefficients(dots[6 * i:6 * i + 6]) for i in range(len(fields))]
 
         if turn == STEPS:
@@ -536,35 +536,39 @@
                 return total
 
             for z in range(parts):
-                lanes = slice(z * LANES, (z + 1) * LANES)
                 line = heads_p[0, x, z, own, :] if turn < 2 else base[x, z, own, :]
-                if with_p:
-                    v = basis(0, z)
-                    rise = combine(coeff[0][0], v)
-                    change = combine(coeff[0][1], v)
-                    before = p0[x, z, own, :] if turn == 0 else sums[0, i, z]
-                    if turn + 1 < STEPS:
-                        sums[0, i, z] = before + rise
-                        heads_p[turn + 1, x, z, own, :] = v[0] - change
-                    else:
-                        result[0, i, :, lanes] = before + rise
+                v = basis(0, z)
+                change = combine(coeff[0][1], v)
+                if turn + 1 < STEPS:
+                    heads_p[turn + 1, x, z, own, :] = v[0] - change
                 if with_c:
-                    v = basis(len(fields) - 1, z)
-                    rise = combine(coeff[-1][0], v)
-                    before = p0[x, z, own, :] if turn == 1 else sums[1, i, z]
-                    sums[1, i, z] = before + rise
-                    line = line - combine(coeff[-1][1], v)
+                    line = line - combine(coeff[1][1], basis(1, z))
                     if turn + 1 < STEPS:
                         base[x, z, own, :] = line
                 heads_c[turn, x, z, own, :] = line + 0.5 * change
             return carry
 
+        def settle(turn=turn, with_c=with_c, fields=fields, coeff=coeff):
+            def rise(i, carry):
+                x = i + PX
+                for z in range(parts):
+                    for f, (head, work) in enumerate(fields):
+                        before = p0[x, z, own, :] if turn == f else sums[f, i, z]
+                        total = coeff[f][0][0] * head[x, z, own, :]
+                        for k in range(1, ITERS):
+                            total = total + coeff[f][0][k] * work[k - 1, x, z, own, :]
+                        if f == 0 and turn + 1 == STEPS:
+                            result[0, i, :, slice(z * LANES, (z + 1) * LANES)] = before + total
+                        else:
+                            sums[f, i, z] = before + total
+                return carry
+
+            lax.fori_loop(0, half, rise, 0, unroll=True)
+
         lax.fori_loop(0, half, update, 0, unroll=True)
         for item in outer:
             wait_halo(item)
         rim(turn, coeff, fields, far)
-        if turn == STEPS - 1:
-            deliver(0)
         used += len(fields)
     for item in pending:
         end_halo(item)

time: 43.7 us -> 43.5 us (level)
  no operation moved by 1% of the time
where the time goes in v5:
time: 43.5 us; the launch traced here: 43.4 us
  Pallas kernels  42.6 us (98%)
  local copies, waits for them, and re-layouts  0.8 us (2%)
    pallas_call x1, Pallas kernels, per_device(): pl.pallas_call(functools.partial(body, (levels, nx, ny), stages), out_sha...  42.6 us

profile of v5, /device:TPU:0, one launch (start us, length us, event | category | flops | bytes accessed | tf_op | source)
XLA Modules:
  0.0 43.4 jit_solution(17282912463984462198)
XLA Ops:
  0.0 42.6 %shard_map.37 = f32[1,32,16,256]{3,2,1,0:T(8,128)S(1)} custom-call(f32[32,16,256]{2,1,0:T(8,128)} %init_ref.1, f32[32,16,256]{2,1,0:T(8,128)} %source_ref.1, f32[32,16,256]{2,1,0:T(8,128)} %damp_ref.1), custom_call_target="tpu_custom_call" | custom-call | tf_op jit(solution)/shard_map/pallas_call | solution.py:607
  42.6 0.8 %copy.5 = f32[1,32,16,256]{3,2,1,0:T(8,128)} copy(f32[1,32,16,256]{3,2,1,0:T(8,128)S(1)} %shard_map.37) | data formatting | bytes 1048576
